TPU v7x, 32 devices: a whole 2x2x4 slice. The times are simulated.
32 devices in a mesh: dp: 2 (over core), tensor: 16 (over z, y, x).
Axes of the slice: x: 2, y: 2, z: 4, core: 2. Of those that a mesh axis runs over, the one named last changes fastest.
Arguments:
- inputs: bfloat16 [768, 6144], P(('dp', 'tensor')), may hold values from -0.29882812 to 0.29882812
- norm_gain: float32 [6144], replicated, may hold values from 0.1 to 1.9
- norm_bias: float32 [6144], replicated, may hold values from -3 to 3
- query_grad: bfloat16 [768, 12288], P('dp', 'tensor'), may hold values from -0.119628906 to 0.119628906
- stream_grad: bfloat16 [768, 6144], P(('dp', 'tensor')), may hold values from -2.390625 to 2.390625
- query_weight: bfloat16 [6144, 12288], P(None, 'tensor'), may hold values from -0.0546875 to 0.0546875
Outputs:
- input_grad: bfloat16 [768, 6144], P(('dp', 'tensor'))
- weight_grad: bfloat16 [6144, 12288], P(None, 'tensor')
All inputs are finite; a program needn't handle non-finite values.
Results may differ from a plain program's by a relative error of at most 0.019.
Values may be sent and summed in bfloat16 or wider, within the bound.
No kernel may reach another device: no remote copies, remote signals or barrier semaphores. Data moves between devices by JAX's collectives and lax.ppermute only.
A program may use at most 128 MiB of HBM per device.

v0:
```python
import jax
import jax.numpy as jnp
from jax import lax
from jax.sharding import PartitionSpec as P

epsilon = 1e-05


def normalize(values, norm_gain, norm_bias):
    as_float = values.astype(jnp.float32)
    centre = jnp.mean(as_float, axis=-1, keepdims=True)
    offsets = as_float - centre
    variance = jnp.mean(offsets * offsets, axis=-1, keepdims=True)
    inverse = lax.rsqrt(variance + epsilon)
    scaled = offsets * inverse
    normed = (scaled * norm_gain + norm_bias).astype(jnp.bfloat16)
    return (scaled, inverse, normed)


def norm_backward(scaled, inverse, normed_grad, norm_gain, stream_grad):
    weighted = normed_grad * norm_gain
    first_moment = jnp.mean(weighted, axis=-1, keepdims=True)
    second_moment = jnp.mean(weighted * scaled, axis=-1, keepdims=True)
    result = stream_grad.astype(jnp.float32) + inverse * (
        weighted - first_moment - scaled * second_moment
    )
    return result.astype(jnp.bfloat16)


def shards(inputs, norm_gain, norm_bias, query_grad, stream_grad, query_weight):
    scaled, inverse, normed = normalize(inputs, norm_gain, norm_bias)
    unused_scaled, unused_inverse, piece_normed = normalize(
        lax.all_gather(inputs, "tensor", axis=0, tiled=True), norm_gain, norm_bias
    )
    grad_rows = query_grad
    weight_grad = lax.psum(
        lax.dot_general(
            piece_normed, grad_rows, (((0,), (0,)), ((), ())), preferred_element_type=jnp.float32
        ).astype(jnp.bfloat16),
        "dp",
    )
    grad_rows = query_grad
    normed_grad = lax.psum_scatter(
        lax.dot_general(
            grad_rows, query_weight, (((1,), (1,)), ((), ())), preferred_element_type=jnp.float32
        ).astype(jnp.bfloat16),
        "tensor",
        scatter_dimension=0,
        tiled=True,
    ).astype(jnp.float32)
    input_grad = norm_backward(scaled, inverse, normed_grad, norm_gain, stream_grad)
    return (input_grad, weight_grad)


def solution(mesh):
    placed = (
        P(("dp", "tensor"), None),
        P(),
        P(),
        P("dp", "tensor"),
        P(("dp", "tensor"), None),
        P(None, "tensor"),
    )
    return jax.shard_map(
        shards,
        mesh=mesh,
        in_specs=placed,
        out_specs=(P(("dp", "tensor"), None), P(None, "tensor")),
        check_vma=False,
    )
```

profile of v0, /device:TPU:0, one launch (start us, length us, event | category | flops | bytes accessed | tf_op | source)
XLA Modules:
  0.0 294.0 jit_solution(8488594455797029391)
XLA Ops:
  7.2 0.0 copy-start
  7.2 0.0 all-gather.2.cloned.1.call-start
  7.2 0.7 all-gather.2.cloned.1.call-update
  7.9 0.0 reduce-scatter.2.cloned.1.call-start
  8.0 0.3 copy-done
  8.2 11.6 %convolution_convert_fusion.1 = bf16[384,6144]{1,0:T(8,128)(2,1)} fusion(bf16[384,768]{1,0:T(8,128)(2,1)S(1)} %copy-done, bf16[6144,768]{1,0:T(8,128)(2,1)} %param.11), kind=kOutput, calls=%fused_computation.9 | convolution fusion | flops 3626237952 | bytes 14745600 | tf_op jit(solution)/shard_map/dot_general | solution.py:44
  19.8 0.0 copy-start.4
  19.8 0.0 copy-start.5
  19.8 0.0 reduce-scatter.2.cloned.1.call-update
  19.8 0.0 all-reduce.2.cloned.1.call-start
  19.9 73.3 %all-gather.2.cloned.1.call-done = bf16[384,6144]{1,0:T(8,128)(2,1)} async-done(((bf16[24,6144]{1,0:T(8,128)(2,1)}), bf16[384,6144]{1,0:T(8,128)(2,1)}) %all-gather.2.cloned.1.call-update) | async-done | bytes 4718608 | tf_op jit(solution)/shard_map/all_gather | solution.py:33
  93.2 0.0 copy-start.1
  93.2 3.2 %convert_reduce_fusion = f32[384]{0:T(512)S(1)} fusion(bf16[384,6144]{1,0:T(8,128)(2,1)} %all-gather.2.cloned.1.call-done), kind=kLoop, calls=%fused_computation.1 | loop fusion | flops 4718208 | bytes 4720128 | tf_op jit(solution)/shard_map/reduce_sum | solution.py:11
  96.4 3.7 %fusion.2 = f32[384]{0:T(512)S(1)} fusion(bf16[384,6144]{1,0:T(8,128)(2,1)} %all-gather.2.cloned.1.call-done, f32[384]{0:T(512)S(1)} %broadcast_multiply_fusion), kind=kLoop, calls=%fused_computation.5 | loop fusion | flops 9436800 | bytes 4721664 | tf_op jit(solution)/shard_map/reduce_sum | solution.py:13
  100.2 0.0 copy-done.4
  100.2 0.0 copy-done.5
  100.2 0.0 copy-done.1
  100.2 8.1 %convolution_convert_fusion = bf16[6144,768]{1,0:T(8,128)(2,1)} fusion(bf16[384,768]{1,0:T(8,128)(2,1)S(1)} %copy-done, bf16[384,6144]{1,0:T(8,128)(2,1)S(1)} %copy-done.1, f32[6144]{0:T(1024)S(1)} %copy-done.5, f32[6144]{0:T(1024)S(1)} %copy-done.4, f32[384]{0:T(512)S(1)} %add_rsqrt_fusion, f32[384]{0:T(512)S(1)} %broadcast_multiply_fusion), kind=kOutput, calls=%fused_computation.4 | convolution fusion | flops 3642753024 | bytes 14797824 | tf_op jit(solution)/shard_map/dot_general | solution.py:37
  108.3 0.0 copy-start.2
  108.3 0.0 copy-start.3
  108.3 0.0 all-reduce.2.cloned.1.call-update
  108.3 0.9 copy-done.2
  109.2 0.2 convert_reduce_fusion.1
  109.4 0.3 fusion.20
  109.7 126.6 %reduce-scatter.2.cloned.1.call-done = bf16[24,6144]{1,0:T(8,128)(2,1)} async-done(((bf16[384,6144]{1,0:T(8,128)(2,1)}), bf16[24,6144]{1,0:T(8,128)(2,1)}) %reduce-scatter.2.cloned.1.call-update) | async-done | bytes 294928 | tf_op jit(solution)/shard_map/reduce_scatter | solution.py:43
  236.2 1.2 fusion.21
  237.5 0.0 copy-done.3
  237.5 2.0 fusion.19
  239.5 39.9 %all-reduce.2.cloned.1.call-done = bf16[6144,768]{1,0:T(8,128)(2,1)} async-done(((bf16[6144,768]{1,0:T(8,128)(2,1)}), bf16[6144,768]{1,0:T(8,128)(2,1)}) %all-reduce.2.cloned.1.call-update) | async-done | bytes 9437200 | tf_op jit(solution)/shard_map/psum | solution.py:36
  279.4 8.0 %copy.9 = bf16[6144,768]{1,0:T(8,128)(2,1)} copy(bf16[6144,768]{1,0:T(8,128)(2,1)} %all-reduce.2.cloned.1.call-done) | data formatting | bytes 18874368
  (5 shorter events, 0.0 us)
Async XLA Ops:
  7.2 1.1 copy-start
  7.2 86.1 %all-gather.2.cloned.1.call-start = ((), (), s32[]{:S(2)}) async-start(), calls=%async_computation.2 | async-start | bytes 5013504 | tf_op jit(solution)/shard_map/all_gather | solution.py:33
  7.9 228.3 %reduce-scatter.2.cloned.1.call-start = ((), (), s32[]{:S(2)}) async-start(), calls=%async_computation.1 | async-start | bytes 5013504 | tf_op jit(solution)/shard_map/reduce_scatter | solution.py:43
  19.8 80.3 %copy-start.4 = (f32[6144]{0:T(1024)S(1)}, f32[6144]{0:T(1024)}, u32[]{:S(2)}) copy-start(f32[6144]{0:T(1024)} %param.7) | copy-start | bytes 73732
  19.8 80.4 %copy-start.5 = (f32[6144]{0:T(1024)S(1)}, f32[6144]{0:T(1024)}, u32[]{:S(2)}) copy-start(f32[6144]{0:T(1024)} %param.8) | copy-start | bytes 73732
  19.8 259.6 %all-reduce.2.cloned.1.call-start = ((), (), s32[]{:S(2)}) async-start(), calls=%async_computation.3 | async-start | bytes 18874368 | tf_op jit(solution)/shard_map/psum | solution.py:36
  93.2 6.9 %copy-start.1 = (bf16[384,6144]{1,0:T(8,128)(2,1)S(1)}, bf16[384,6144]{1,0:T(8,128)(2,1)}, u32[]{:S(2)}) copy-start(bf16[384,6144]{1,0:T(8,128)(2,1)} %all-gather.2.cloned.1.call-done) | copy-start | bytes 14155780
  108.3 1.0 copy-start.2
  108.3 129.2 %copy-start.3 = (bf16[24,6144]{1,0:T(8,128)(2,1)S(1)}, bf16[24,6144]{1,0:T(8,128)(2,1)}, u32[]{:S(2)}) copy-start(bf16[24,6144]{1,0:T(8,128)(2,1)} %param.10) | copy-start | bytes 884740
Sparse Core Ops, SparseCore 0:
  10.8 82.3 all-gather.1
  98.4 137.8 reduce-scatter.1
  239.3 40.0 all-reduce.1
where the time goes:
time: 294 us
  waiting for transfers between devices  241 us (82%)
  matrix products  19.7 us (7%)
  between operations  13.8 us (5%)
  other arithmetic  10.6 us (4%)
  local copies, waits for them, and re-layouts  9.26 us (3%)
    reduce_scatter x1, waiting for transfers between devices, shards(): lax.psum_scatter(lax.dot_general(grad_rows, query_weight, (((1,), (1,)),...  127 us
    all_gather x1, waiting for transfers between devices, shards(): lax.all_gather(inputs, 'tensor', axis=0, tiled=True)  73.3 us
    psum x1, waiting for transfers between devices, shards(): lax.psum(lax.dot_general(piece_normed, grad_rows, (((0,), (0,)), ((), ())...  39.9 us
    dot_general x1, matrix products, shards(): lax.dot_general(grad_rows, query_weight, (((1,), (1,)), ((), ())), prefer...  11.6 us
    unnamed x13, local copies, waits for them, and re-layouts  9.26 us
    dot_general x1, matrix products, shards(): lax.dot_general(piece_normed, grad_rows, (((0,), (0,)), ((), ())), prefer...  8.08 us
  transfers between devices with their start and end apart: 3, of which 3 were waited for; matrix products, arithmetic and copies ran while one was open for 10% of the time, Pallas kernels for 0%

commit v1 on v0

--- a/solution.py
+++ b/solution.py
@@ -33,12 +33,11 @@
         lax.all_gather(inputs, "tensor", axis=0, tiled=True), norm_gain, norm_bias
     )
     grad_rows = query_grad
-    weight_grad = lax.psum(
-        lax.dot_general(
-            piece_normed, grad_rows, (((0,), (0,)), ((), ())), preferred_element_type=jnp.float32
-        ).astype(jnp.bfloat16),
-        "dp",
-    )
+    message = lax.dot_general(
+        piece_normed, grad_rows, (((0,), (0,)), ((), ())), preferred_element_type=jnp.float32
+    ).astype(jnp.bfloat16)
+    reached = jax.lax.all_gather(message, axis_name="dp")
+    weight_grad = jnp.sum(reached, axis=0)
     grad_rows = query_grad
     normed_grad = lax.psum_scatter(
         lax.dot_general(

time: 294 us -> 295 us (level)
  other arithmetic: 10.6 us -> 27.4 us
  waiting for transfers between devices: 241 us -> 232 us
  local copies, waits for them, and re-layouts: 9.26 us -> 1.23 us
    psum x1 -> x0, waiting for transfers between devices: 39.9 us -> none  [shards(): lax.psum(lax.dot_general(piece_normed, grad_rows, (((0,), (0,)), ((), ())...]
    all_gather x0 -> x1, waiting for transfers between devices: none -> 31.5 us  [shards(): reached = jax.lax.all_gather(message, axis_name='dp')]
    reduce_sum x0 -> x1, other arithmetic: none -> 16.8 us  [shards(): weight_grad = jnp.sum(reached, axis=0)]
    unnamed x13 -> x12, local copies, waits for them, and re-layouts: 9.26 us -> 1.23 us
where the time goes in v1:
time: 295 us; the launch traced here: 294 us
  waiting for transfers between devices  232 us (79%)
  other arithmetic  27.4 us (9%)
  matrix products  19.6 us (7%)
  between operations  13.8 us (5%)
    reduce_scatter x1, waiting for transfers between devices, shards(): lax.psum_scatter(lax.dot_general(grad_rows, query_weight, (((1,), (1,)),...  127 us
    all_gather x1, waiting for transfers between devices, shards(): lax.all_gather(inputs, 'tensor', axis=0, tiled=True)  73.4 us
    all_gather x1, waiting for transfers between devices, shards(): reached = jax.lax.all_gather(message, axis_name='dp')  31.5 us
    reduce_sum x1, other arithmetic, shards(): weight_grad = jnp.sum(reached, axis=0)  16.8 us
    dot_general x1, matrix products, shards(): lax.dot_general(grad_rows, query_weight, (((1,), (1,)), ((), ())), prefer...  11.5 us
    dot_general x1, matrix products, shards(): lax.dot_general(piece_normed, grad_rows, (((0,), (0,)), ((), ())), prefer...  8.08 us
  transfers between devices with their start and end apart: 3, of which 3 were waited for; matrix products, arithmetic and copies ran while one was open for 10% of the time, Pallas kernels for 0%

profile of v1, /device:TPU:0, one launch (start us, length us, event | category | flops | bytes accessed | tf_op | source)
XLA Modules:
  0.0 294.4 jit_solution(16958586223890224192)
XLA Ops:
  7.2 0.0 copy-start
  7.2 0.0 all-gather.4.cloned.1.call-start
  7.2 0.7 all-gather.4.cloned.1.call-update
  7.9 0.0 reduce-scatter.2.cloned.1.call-start
  8.0 0.3 copy-done
  8.2 11.5 %convolution_convert_fusion.1 = bf16[384,6144]{1,0:T(8,128)(2,1)} fusion(bf16[384,768]{1,0:T(8,128)(2,1)S(1)} %copy-done, bf16[6144,768]{1,0:T(8,128)(2,1)} %param.11), kind=kOutput, calls=%fused_computation.9 | convolution fusion | flops 3626237952 | bytes 14745600 | tf_op jit(solution)/shard_map/dot_general | solution.py:43
  19.8 0.0 copy-start.4
  19.8 0.0 copy-start.5
  19.8 0.0 reduce-scatter.2.cloned.1.call-update
  19.8 0.0 all-gather.6.cloned.1.call-start
  19.8 73.4 %all-gather.4.cloned.1.call-done = bf16[384,6144]{1,0:T(8,128)(2,1)} async-done(((bf16[24,6144]{1,0:T(8,128)(2,1)}), bf16[384,6144]{1,0:T(8,128)(2,1)}) %all-gather.4.cloned.1.call-update) | async-done | bytes 4718608 | tf_op jit(solution)/shard_map/all_gather | solution.py:33
  93.2 0.0 copy-start.1
  93.2 3.2 %convert_reduce_fusion = f32[384]{0:T(512)S(1)} fusion(bf16[384,6144]{1,0:T(8,128)(2,1)} %all-gather.4.cloned.1.call-done), kind=kLoop, calls=%fused_computation.1 | loop fusion | flops 4718208 | bytes 4720128 | tf_op jit(solution)/shard_map/reduce_sum | solution.py:11
  96.4 3.7 %fusion.2 = f32[384]{0:T(512)S(1)} fusion(bf16[384,6144]{1,0:T(8,128)(2,1)} %all-gather.4.cloned.1.call-done, f32[384]{0:T(512)S(1)} %broadcast_multiply_fusion), kind=kLoop, calls=%fused_computation.5 | loop fusion | flops 9436800 | bytes 4721664 | tf_op jit(solution)/shard_map/reduce_sum | solution.py:13
  100.2 0.0 copy-done.4
  100.2 0.0 copy-done.5
  100.2 0.0 copy-done.1
  100.2 8.1 %convolution_convert_fusion = bf16[6144,768]{1,0:T(8,128)(2,1)} fusion(bf16[384,768]{1,0:T(8,128)(2,1)S(1)} %copy-done, bf16[384,6144]{1,0:T(8,128)(2,1)S(1)} %copy-done.1, f32[6144]{0:T(1024)S(1)} %copy-done.5, f32[6144]{0:T(1024)S(1)} %copy-done.4, f32[384]{0:T(512)S(1)} %add_rsqrt_fusion, f32[384]{0:T(512)S(1)} %broadcast_multiply_fusion), kind=kOutput, calls=%fused_computation.4 | convolution fusion | flops 3642753024 | bytes 14797824 | tf_op jit(solution)/shard_map/dot_general | solution.py:36
  108.3 0.0 copy-start.2
  108.3 0.0 copy-start.3
  108.3 0.0 all-gather.6.cloned.1.call-update
  108.3 0.9 copy-done.2
  109.2 0.2 convert_reduce_fusion.1
  109.4 0.3 fusion.20
  109.7 126.6 %reduce-scatter.2.cloned.1.call-done = bf16[24,6144]{1,0:T(8,128)(2,1)} async-done(((bf16[384,6144]{1,0:T(8,128)(2,1)}), bf16[24,6144]{1,0:T(8,128)(2,1)}) %reduce-scatter.2.cloned.1.call-update) | async-done | bytes 294928 | tf_op jit(solution)/shard_map/reduce_scatter | solution.py:42
  236.3 1.2 fusion.21
  237.6 0.0 copy-done.3
  237.6 2.0 fusion.19
  239.5 31.5 %all-gather.6.cloned.1.call-done = bf16[12288,768]{1,0:T(8,128)(2,1)} async-done(((bf16[6144,768]{1,0:T(8,128)(2,1)}), bf16[12288,768]{1,0:T(8,128)(2,1)}) %all-gather.6.cloned.1.call-update) | async-done | bytes 18874384 | tf_op jit(solution)/shard_map/all_gather | solution.py:39
  271.0 16.8 %reduce_sum.72 = bf16[6144,768]{1,0:T(8,128)(2,1)} reduce(bf16[2,6144,768]{2,1,0:T(8,128)(2,1)} %bitcast.4, bf16[]{:T(256)} %constant.15.clone.1), dimensions={0}, to_apply=%region_7.0 | reduce | flops 4718592 | bytes 28311554 | tf_op jit(solution)/shard_map/reduce_sum | solution.py:40
  (5 shorter events, 0.0 us)
Async XLA Ops:
  7.2 1.1 copy-start
  7.2 86.1 %all-gather.4.cloned.1.call-start = ((), (), s32[]{:S(2)}) async-start(), calls=%async_computation.2 | async-start | bytes 5013504 | tf_op jit(solution)/shard_map/all_gather | solution.py:33
  7.9 228.4 %reduce-scatter.2.cloned.1.call-start = ((), (), s32[]{:S(2)}) async-start(), calls=%async_computation.1 | async-start | bytes 5013504 | tf_op jit(solution)/shard_map/reduce_scatter | solution.py:42
  19.8 80.4 %copy-start.4 = (f32[6144]{0:T(1024)S(1)}, f32[6144]{0:T(1024)}, u32[]{:S(2)}) copy-start(f32[6144]{0:T(1024)} %param.7) | copy-start | bytes 73732
  19.8 80.4 %copy-start.5 = (f32[6144]{0:T(1024)S(1)}, f32[6144]{0:T(1024)}, u32[]{:S(2)}) copy-start(f32[6144]{0:T(1024)} %param.8) | copy-start | bytes 73732
  19.8 251.3 %all-gather.6.cloned.1.call-start = ((), (), s32[]{:S(2)}) async-start(), calls=%async_computation.3 | async-start | bytes 28311552 | tf_op jit(solution)/shard_map/all_gather | solution.py:39
  93.2 6.9 %copy-start.1 = (bf16[384,6144]{1,0:T(8,128)(2,1)S(1)}, bf16[384,6144]{1,0:T(8,128)(2,1)}, u32[]{:S(2)}) copy-start(bf16[384,6144]{1,0:T(8,128)(2,1)} %all-gather.4.cloned.1.call-done) | copy-start | bytes 14155780
  108.3 1.0 copy-start.2
  108.3 129.3 %copy-start.3 = (bf16[24,6144]{1,0:T(8,128)(2,1)S(1)}, bf16[24,6144]{1,0:T(8,128)(2,1)}, u32[]{:S(2)}) copy-start(bf16[24,6144]{1,0:T(8,128)(2,1)} %param.10) | copy-start | bytes 884740
Sparse Core Ops, SparseCore 0:
  10.8 82.3 all-gather.3
  98.4 137.8 reduce-scatter.1
  238.4 32.5 all-gather.5
